TPU v7x, 256 devices: a whole 4x4x8 slice. The times are simulated.
256 devices in a mesh: samp: 64 (over y, z, core), var: 4 (over x).
Axes of the slice: x: 4, y: 4, z: 8, core: 2. Of those that a mesh axis runs over, the one named last changes fastest.
Arguments:
- phenotype: float32 [65536], replicated, may hold values from -6 to 6
- perm_index: int32 [64, 65536], P(None, 'samp'), may hold values from 0 to 65535, each once within a row
- genotypes: bfloat16 [65536, 8192], P('samp', 'var'), may hold values from 0 to 2
Outputs:
- statistics: float32 [64, 8192], P('samp', 'var')
- largest: float32 [64], P('samp')
Inputs may be any that keep to these rules, and one draw needn't show every extreme that they name: Each row of perm_index is a permutation of 0 to 65535.
All inputs are finite; a program needn't handle non-finite values.
Results may differ from a plain program's by a relative error of at most 0.003.
Values sent between devices are 32-bit elements; how exact they have to be, the bound alone decides.
A program may use at most 64 MiB of HBM per device.

v0:
```python
import jax
import jax.numpy as jnp
from jax import lax
from jax.sharding import PartitionSpec as P


def split_up(shard, dim, length):
    dims = shard.shape
    pieces = shard.reshape(*dims[:dim], length, dims[dim] // length, *dims[dim + 1 :])
    return jnp.moveaxis(pieces, dim, 0)


def sent_and_summed(shard, axis, dim):
    pieces = split_up(shard, dim, lax.axis_size(axis))
    arrived = lax.all_to_all(pieces, axis, split_axis=0, concat_axis=0, tiled=True)
    return arrived.sum(axis=0)


def from_everyone(shard, axis):
    length = lax.axis_size(axis)
    return lax.all_to_all(
        jnp.broadcast_to(shard[None], (length, *shard.shape)), axis, 0, 0, tiled=True
    )


def over_copies(shard, axis):
    everything = from_everyone(shard, axis)
    return jnp.sum(everything, axis=0)


def over_copies_2(shard, axis):
    everything = from_everyone(shard, axis)
    return jnp.max(everything, axis=0)


def on_device(phenotype, perm_index, genotypes):
    centred = phenotype - jnp.mean(phenotype)
    sigma2 = jnp.mean(centred * centred) + 1e-05
    local_count = perm_index.shape[1]
    perm_total = perm_index.shape[0]
    table = centred.astype(jnp.bfloat16).reshape(centred.shape[0] // 128, 128)

    def select_rows(index_rows):
        upper_part = jax.nn.one_hot(index_rows // 128, table.shape[0], dtype=jnp.bfloat16)
        picked = jnp.einsum("pnh,hc->pnc", upper_part, table, preferred_element_type=jnp.float32)
        lower_part = jax.nn.one_hot(index_rows % 128, 128, dtype=jnp.float32)
        return jnp.sum(picked * lower_part, axis=-1).astype(jnp.bfloat16)

    grouped = perm_index.reshape(perm_total // 8, 8, local_count)
    permuted = lax.map(select_rows, grouped).reshape(perm_total, local_count)
    ones_row = jnp.ones((1, genotypes.shape[0]), jnp.bfloat16)
    count_row = jnp.dot(ones_row, genotypes, preferred_element_type=jnp.float32)
    square_row = jnp.einsum("ij,ij->j", genotypes, genotypes, preferred_element_type=jnp.float32)[
        None, :
    ]
    moments = jnp.concatenate([count_row, square_row], axis=0)
    samples = local_count * lax.axis_size("samp")
    own_scores = sent_and_summed(
        jnp.dot(permuted, genotypes, preferred_element_type=jnp.float32), "samp", 0
    )
    totals = over_copies(moments, "samp")
    spread = totals[1] - totals[0] * totals[0] / samples + 1.0
    statistic = own_scores / jnp.sqrt(sigma2 * spread)[None, :]
    largest = over_copies_2(jnp.max(jnp.abs(statistic), axis=1), "var")
    return (statistic, largest)


def solution(mesh):
    placed = (P(), P(None, "samp"), P("samp", "var"))
    return jax.shard_map(
        on_device,
        mesh=mesh,
        in_specs=placed,
        out_specs=(P("samp", "var"), P("samp")),
        check_vma=False,
    )
```

profile of v0, /device:TPU:1, one launch (start us, length us, event | category | flops | bytes accessed | tf_op | source)
XLA Modules:
  0.0 137.3 jit_solution(2388754105524033553)
XLA Ops:
  0.6 1.6 %reduce_sum.50 = f32[]{:T(128)} reduce(f32[65536]{0:T(1024)} %param.5, f32[]{:T(128)} %constant.77.clone.1), dimensions={0}, to_apply=%region_0.0 | reduce | flops 65535 | bytes 262152 | tf_op jit(solution)/shard_map/reduce_sum | solution.py:37
  2.9 1.6 %multiply_reduce_fusion = (f32[]{:T(128)}, bf16[512,128]{1,0:T(8,128)(2,1)S(1)}) fusion(f32[65536]{0:T(1024)} %param.5, f32[]{:T(128)S(6)} %div.30), kind=kLoop, calls=%fused_computation.20 | loop fusion | flops 262143 | bytes 393224 | tf_op jit(solution)/shard_map/reduce_sum | solution.py:38
  4.7 50.7 %while.12 = (s32[]{:T(128)}, bf16[8,8,1024]{2,1,0:T(8,128)(2,1)S(1)}, s32[8,8,1024]{2,1,0:T(8,128)}, bf16[512,128]{0,1:T(8,128)(2,1)S(1)}, s32[]{:T(128)}) while((s32[]{:T(128)}, bf16[8,8,1024]{2,1,0:T(8,128)(2,1)S(1)}, s32[8,8,1024]{2,1,0:T(8,128)}, bf16[512,128]{0,1:T(8,128)(2,1)S(1)}, s32[]{:T(128)}) %tuple.42), condition=%wide.region_3.4_spmd, body=%wide.region_1.3_spmd.sunk | while | flops 1081278464 | bytes 393297 | solution.py:50
  6.2 4.7 %select_reduce_fusion.2 = bf16[8,1024]{1,0:T(8,128)(2,1)S(1)} fusion(s32[8,1024]{1,0:T(8,128)S(1)} %add_select_fusion.5, s32[8,1024]{1,0:T(8,128)S(1)} %get-tuple-element.117, bf16[512,128]{0,1:T(8,128)(2,1)S(1)} %get-tuple-element.131), kind=kOutput, calls=%fused_computation.3.clone.1 | convolution fusion | flops 1081073664 | bytes 212992 | tf_op jit(solution)/shard_map/while/body/eval_jaxpr/pnh,hc->pnc/dot_general | solution.py:45
  12.6 4.7 %select_reduce_fusion.2 = bf16[8,1024]{1,0:T(8,128)(2,1)S(1)} fusion(s32[8,1024]{1,0:T(8,128)S(1)} %add_select_fusion.5, s32[8,1024]{1,0:T(8,128)S(1)} %get-tuple-element.117, bf16[512,128]{0,1:T(8,128)(2,1)S(1)} %get-tuple-element.131), kind=kOutput, calls=%fused_computation.3.clone.1 | convolution fusion | flops 1081073664 | bytes 212992 | tf_op jit(solution)/shard_map/while/body/eval_jaxpr/pnh,hc->pnc/dot_general | solution.py:45
  17.4 0.8 add_select_fusion.4
  18.9 4.7 %select_reduce_fusion.2 = bf16[8,1024]{1,0:T(8,128)(2,1)S(1)} fusion(s32[8,1024]{1,0:T(8,128)S(1)} %add_select_fusion.5, s32[8,1024]{1,0:T(8,128)S(1)} %get-tuple-element.117, bf16[512,128]{0,1:T(8,128)(2,1)S(1)} %get-tuple-element.131), kind=kOutput, calls=%fused_computation.3.clone.1 | convolution fusion | flops 1081073664 | bytes 212992 | tf_op jit(solution)/shard_map/while/body/eval_jaxpr/pnh,hc->pnc/dot_general | solution.py:45
  25.3 4.7 %select_reduce_fusion.2 = bf16[8,1024]{1,0:T(8,128)(2,1)S(1)} fusion(s32[8,1024]{1,0:T(8,128)S(1)} %add_select_fusion.5, s32[8,1024]{1,0:T(8,128)S(1)} %get-tuple-element.117, bf16[512,128]{0,1:T(8,128)(2,1)S(1)} %get-tuple-element.131), kind=kOutput, calls=%fused_computation.3.clone.1 | convolution fusion | flops 1081073664 | bytes 212992 | tf_op jit(solution)/shard_map/while/body/eval_jaxpr/pnh,hc->pnc/dot_general | solution.py:45
  31.6 4.7 %select_reduce_fusion.2 = bf16[8,1024]{1,0:T(8,128)(2,1)S(1)} fusion(s32[8,1024]{1,0:T(8,128)S(1)} %add_select_fusion.5, s32[8,1024]{1,0:T(8,128)S(1)} %get-tuple-element.117, bf16[512,128]{0,1:T(8,128)(2,1)S(1)} %get-tuple-element.131), kind=kOutput, calls=%fused_computation.3.clone.1 | convolution fusion | flops 1081073664 | bytes 212992 | tf_op jit(solution)/shard_map/while/body/eval_jaxpr/pnh,hc->pnc/dot_general | solution.py:45
  36.4 0.8 add_select_fusion.4
  37.9 4.7 %select_reduce_fusion.2 = bf16[8,1024]{1,0:T(8,128)(2,1)S(1)} fusion(s32[8,1024]{1,0:T(8,128)S(1)} %add_select_fusion.5, s32[8,1024]{1,0:T(8,128)S(1)} %get-tuple-element.117, bf16[512,128]{0,1:T(8,128)(2,1)S(1)} %get-tuple-element.131), kind=kOutput, calls=%fused_computation.3.clone.1 | convolution fusion | flops 1081073664 | bytes 212992 | tf_op jit(solution)/shard_map/while/body/eval_jaxpr/pnh,hc->pnc/dot_general | solution.py:45
  44.3 4.7 %select_reduce_fusion.2 = bf16[8,1024]{1,0:T(8,128)(2,1)S(1)} fusion(s32[8,1024]{1,0:T(8,128)S(1)} %add_select_fusion.5, s32[8,1024]{1,0:T(8,128)S(1)} %get-tuple-element.117, bf16[512,128]{0,1:T(8,128)(2,1)S(1)} %get-tuple-element.131), kind=kOutput, calls=%fused_computation.3.clone.1 | convolution fusion | flops 1081073664 | bytes 212992 | tf_op jit(solution)/shard_map/while/body/eval_jaxpr/pnh,hc->pnc/dot_general | solution.py:45
  50.6 4.7 %select_reduce_fusion.2 = bf16[8,1024]{1,0:T(8,128)(2,1)S(1)} fusion(s32[8,1024]{1,0:T(8,128)S(1)} %add_select_fusion.5, s32[8,1024]{1,0:T(8,128)S(1)} %get-tuple-element.117, bf16[512,128]{0,1:T(8,128)(2,1)S(1)} %get-tuple-element.131), kind=kOutput, calls=%fused_computation.3.clone.1 | convolution fusion | flops 1081073664 | bytes 212992 | tf_op jit(solution)/shard_map/while/body/eval_jaxpr/pnh,hc->pnc/dot_general | solution.py:45
  55.4 3.0 %convolution_bitcast_fusion = f32[64,1,2048]{2,0,1:T(8,128)S(1)} fusion(bf16[1024,2048]{1,0:T(8,128)(2,1)} %param.7, bf16[8,8,1024]{2,1,0:T(8,128)(2,1)S(1)} %get-tuple-element.58), kind=kOutput, calls=%fused_computation.19 | convolution fusion | flops 268435456 | bytes 4849664 | tf_op jit(solution)/shard_map/dot_general | solution.py:59
  58.4 1.3 copy.11
  59.8 13.1 %all-to-all-start = ((f32[64,1,2048]{2,1,0:T(1,128)}), f32[64,1,2048]{2,1,0:T(1,128)S(1)}, u32[]{:S(2)}, u32[]{:S(2)}) async-start(f32[64,1,2048]{2,1,0:T(1,128)} %copy.11), calls=%async_computation | async-start | bytes 1048576 | tf_op jit(solution)/shard_map/all_to_all | solution.py:15
  72.9 3.0 %fusion.11 = f32[1,2048]{1,0:T(1,128)S(1)} fusion(bf16[1024,2048]{1,0:T(8,128)(2,1)} %param.7), kind=kOutput, calls=%fused_computation.30 | convolution fusion | flops 4194304 | bytes 4202496 | tf_op jit(solution)/shard_map/dot_general | solution.py:52
  76.4 0.9 fusion.6
  77.3 12.9 %all-to-all-done = f32[64,1,2048]{2,1,0:T(1,128)S(1)} async-done(((f32[64,1,2048]{2,1,0:T(1,128)}), f32[64,1,2048]{2,1,0:T(1,128)S(1)}, u32[]{:S(2)}, u32[]{:S(2)}) %all-to-all-start) | async-done | bytes 524320 | tf_op jit(solution)/shard_map/all_to_all | solution.py:15
  90.2 1.5 %broadcast_in_dim.31 = f32[64,2,2048]{2,1,0:T(2,128)} broadcast(f32[2,2048]{1,0:T(2,128)S(1)} %pad_maximum_fusion), dimensions={1,2} | broadcast | bytes 1064960 | tf_op jit(solution)/shard_map/broadcast_in_dim | solution.py:22
  91.7 6.3 %all-to-all-start.1 = ((f32[64,2,2048]{2,1,0:T(2,128)}), f32[64,2,2048]{2,1,0:T(2,128)S(1)}, u32[]{:S(2)}, u32[]{:S(2)}) async-start(f32[64,2,2048]{2,1,0:T(2,128)} %broadcast_in_dim.31), calls=%async_computation.1 | async-start | bytes 2097152 | tf_op jit(solution)/shard_map/all_to_all | solution.py:21
  99.0 27.6 %all-to-all-done.1 = f32[64,2,2048]{2,1,0:T(2,128)S(1)} async-done(((f32[64,2,2048]{2,1,0:T(2,128)}), f32[64,2,2048]{2,1,0:T(2,128)S(1)}, u32[]{:S(2)}, u32[]{:S(2)}) %all-to-all-start.1) | async-done | bytes 1048608 | tf_op jit(solution)/shard_map/all_to_all | solution.py:21
  126.9 1.2 abs_reduce_fusion
  128.7 7.9 %all_to_all.16 = f32[4,1,1]{2,1,0:T(1,128)S(1)} all-to-all(f32[4,1,1]{2,1,0:T(1,128)S(1)} %broadcast_in_dim.32), channel_id=1, replica_groups=mesh['samp'=64,'var'=4] {'var'}, dimensions={0} | all-to-all | bytes 32 | tf_op jit(solution)/shard_map/all_to_all | solution.py:21
  (31 shorter events, 13.5 us)
Async XLA Ops:
  59.8 30.4 %all-to-all-start = ((f32[64,1,2048]{2,1,0:T(1,128)}), f32[64,1,2048]{2,1,0:T(1,128)S(1)}, u32[]{:S(2)}, u32[]{:S(2)}) async-start(f32[64,1,2048]{2,1,0:T(1,128)} %copy.11), calls=%async_computation | async-start | bytes 1048576 | tf_op jit(solution)/shard_map/all_to_all | solution.py:15
  72.9 3.5 %copy-start = (bf16[1024,2048]{1,0:T(8,128)(2,1)S(1)}, bf16[1024,2048]{1,0:T(8,128)(2,1)}, u32[]{:S(2)}) copy-start(bf16[1024,2048]{1,0:T(8,128)(2,1)} %param.7) | copy-start | bytes 12582916
  91.7 34.8 %all-to-all-start.1 = ((f32[64,2,2048]{2,1,0:T(2,128)}), f32[64,2,2048]{2,1,0:T(2,128)S(1)}, u32[]{:S(2)}, u32[]{:S(2)}) async-start(f32[64,2,2048]{2,1,0:T(2,128)} %broadcast_in_dim.31), calls=%async_computation.1 | async-start | bytes 2097152 | tf_op jit(solution)/shard_map/all_to_all | solution.py:21
where the time goes:
time: 139 us; the launch traced here: 137 us
  matrix products  43.8 us (32%)
  waiting for transfers between devices  40.5 us (29%)
  starting transfers between devices  19.4 us (14%)
  other arithmetic  19.2 us (14%)
  blocking collectives  7.95 us (6%)
  local copies, waits for them, and re-layouts  4.1 us (3%)
  between operations  2 us (1%)
    dot_general x8, matrix products, select_rows(): jnp.einsum('pnh,hc->pnc', upper_part, table, preferred_element_type=jnp.f...  37.8 us
    all_to_all x1, waiting for transfers between devices, from_everyone(): lax.all_to_all(jnp.broadcast_to(shard[None], (length, *shard.shape)), axi...  27.6 us
    all_to_all x1, starting transfers between devices, sent_and_summed(): lax.all_to_all(pieces, axis, split_axis=0, concat_axis=0, tiled=True)  13.1 us
    all_to_all x1, waiting for transfers between devices, sent_and_summed(): lax.all_to_all(pieces, axis, split_axis=0, concat_axis=0, tiled=True)  12.9 us
    all_to_all x1, blocking collectives, from_everyone(): lax.all_to_all(jnp.broadcast_to(shard[None], (length, *shard.shape)), axi...  7.95 us
    select_n x8, other arithmetic, select_rows(): index_rows // 128  6.3 us
    all_to_all x1, starting transfers between devices, from_everyone(): lax.all_to_all(jnp.broadcast_to(shard[None], (length, *shard.shape)), axi...  6.29 us
    select_n x8, other arithmetic, select_rows(): lower_part = jax.nn.one_hot(index_rows % 128, 128, dtype=jnp.float32)  6.25 us
  transfers between devices with their start and end apart: 2, of which 2 were waited for; matrix products, arithmetic and copies ran while one was open for 3% of the time, Pallas kernels for 0%

commit v1 on v0

v1 whole, which is shorter than its diff:
```python
import functools

import jax
import jax.numpy as jnp
from jax import lax
from jax.experimental import pallas as pl
from jax.experimental.pallas import tpu as pltpu
from jax.sharding import PartitionSpec as P

MESH = pl.DeviceIdType.MESH
F32 = jnp.float32
BF16 = jnp.bfloat16
CHUNKS = 4
G_COPIES = 4


def kernel(dims, phen_hbm, idx_hbm, g_hbm, stat_out, max_out, phen, table, idx, g, perm, perm16, scores, from_core,
           chip_sum, from_y, y_sum, from_z, mom, mom_core, mom_y, mom_y_sum, mom_z, top, from_x, local_sem, ag_send,
           ag_recv, mom_send, mom_recv, core_send, core_recv, y_send, y_recv, z_send, z_recv, x_send, x_recv):
    ny, nz, nx = dims
    local = idx.shape[1]
    columns = g.shape[1]
    width = columns // CHUNKS
    lanes = columns // 128
    samples = phen.shape[0] * 128
    s = lax.axis_index("samp")
    v = lax.axis_index("var")
    core = lax.rem(s, 2)
    z = lax.rem(lax.div(s, 2), nz)
    y = lax.div(s, 2 * nz)

    def at(yy, zz, cc, vv):
        return ((yy * nz + zz) * 2 + cc, vv)

    def y_peer(d):
        return lax.rem(y + d, ny)

    def z_peer(d):
        return lax.rem(z + d, nz)

    def x_peer(d):
        return lax.rem(v + d, nx)

    partner = at(y, z, 1 - core, v)
    peers = [partner]
    peers += [at(y_peer(d), z, core, v) for d in range(1, ny)]
    peers += [at(y, z_peer(d), core, v) for d in range(1, nz)]
    peers += [at(y, z, core, x_peer(d)) for d in range(1, nx)]

    own_core = lax.div(v, nx // 2)
    own_y = lax.rem(v, nx // 2) * (2 * ny // nx)
    rows = idx.shape[0]

    phen_copy = pltpu.make_async_copy(phen_hbm, phen, local_sem.at[0])
    phen_copy.start()
    idx_copy = pltpu.make_async_copy(
        idx_hbm.at[pl.ds(pl.multiple_of(own_y * 2 * nz, 8), rows), :], idx, local_sem.at[1]
    )
    idx_copy.start()
    step = local // G_COPIES
    g_copies = [
        pltpu.make_async_copy(g_hbm.at[pl.ds(k * step, step), :], g.at[pl.ds(k * step, step), :], local_sem.at[2 + k])
        for k in range(G_COPIES)
    ]
    for copy in g_copies:
        copy.start()

    barrier = pltpu.get_barrier_semaphore()
    for peer in peers:
        pl.semaphore_signal(barrier, inc=1, device_id=peer, device_id_type=MESH)

    phen_copy.wait()
    trait = phen[...]
    mean = jnp.sum(trait, keepdims=True) / samples
    centred = trait - mean
    sigma2 = jnp.sum(centred * centred, keepdims=True) / samples + 1e-05
    half = phen.shape[0] // 2
    table[:, :128] = centred[:half].astype(BF16)
    table[:, 128:] = centred[half:].astype(BF16)
    idx_copy.wait()

    sent = []

    def send(src, dst, send_sem, recv_sem, peer):
        copy = pltpu.make_async_remote_copy(
            src_ref=src, dst_ref=dst, send_sem=send_sem, recv_sem=recv_sem, device_id=peer, device_id_type=MESH
        )
        copy.start()
        sent.append(copy)
        return copy

    places = lax.broadcasted_iota(jnp.int32, (256, 256), 0)
    own_rows = rows // 2
    base = v * own_rows
    ag = []
    for block in range(own_rows // 8):

        def look_up(k, carry):
            index = idx[pl.ds(2 * (block * 8 + k) + own_core, 1), :]
            inner = (index & 127) | ((index >> 15) << 7)
            outer = (index >> 7) & 255
            for start in range(0, local, 256):
                one_hot = jnp.where(places == inner[:, start : start + 256], 1.0, 0.0).astype(BF16)
                picked = jnp.dot(table[...], one_hot, preferred_element_type=F32)
                chosen = jnp.where(places == outer[:, start : start + 256], picked, 0.0)
                perm[pl.ds(base + block * 8 + k, 1), start : start + 256] = jnp.sum(chosen, axis=0, keepdims=True)
            return carry

        lax.fori_loop(0, 8, look_up, 0)
        if block == 0:
            pl.semaphore_wait(barrier, len(peers))
        part = perm.at[pl.ds(pl.multiple_of(base + block * 8, 8), 8), :]
        for d in range(1, nx):
            ag.append(
                send(part, part, ag_send.at[d - 1, block], ag_recv.at[d - 1, block], at(y, z, core, x_peer(d)))
            )

    for copy in g_copies:
        copy.wait()
    for block in range(columns // 256):

        def add_rows(i, sums):
            piece = g[pl.ds(pl.multiple_of(i * 64, 64), 64), block * 256 : (block + 1) * 256].astype(F32)
            piece = piece.reshape(8, 8, 256)
            return sums[0] + jnp.sum(piece, axis=0), sums[1] + jnp.sum(piece * piece, axis=0)

        zero = jnp.zeros((8, 256), F32)
        sums = lax.fori_loop(0, local // 64, add_rows, (zero, zero))
        for q in range(2):
            line = jnp.sum(sums[q], axis=0, keepdims=True)
            for j in range(2):
                mom[q, pl.ds(2 * block + j, 1), :] = line[:, j * 128 : (j + 1) * 128]

    mom_copy = send(mom, mom_core, mom_send.at[0], mom_recv.at[0], partner)
    for copy in ag:
        copy.wait_recv()
    perm16[...] = perm[...].astype(BF16)

    mine = core * (ny * nz)
    other = (1 - core) * (ny * nz)
    core_copies = []
    for c in range(CHUNKS):
        cols = pl.ds(c * width, width)
        scores[:, cols] = jnp.dot(perm16[...], g[:, cols], preferred_element_type=F32)
        core_copies.append(
            send(
                scores.at[pl.ds(pl.multiple_of(other, 8), ny * nz), cols],
                from_core.at[:, cols],
                core_send.at[c],
                core_recv.at[c],
                partner,
            )
        )

    mom_copy.wait_recv()
    mom_core[...] = mom[...] + mom_core[...]
    mom_copies = [
        send(mom_core, mom_y.at[d - 1], mom_send.at[d], mom_recv.at[d], at(y_peer(d), z, core, v))
        for d in range(1, ny)
    ]

    y_copies = []
    for c in range(CHUNKS):
        cols = pl.ds(c * width, width)
        core_copies[c].wait_recv()
        chip_sum[:, cols] = scores[pl.ds(pl.multiple_of(mine, 8), ny * nz), cols] + from_core[:, cols]
        y_copies.append([
            send(
                chip_sum.at[pl.ds(pl.multiple_of(y_peer(d) * nz, 8), nz), cols],
                from_y.at[d - 1, :, cols],
                y_send.at[d - 1, c],
                y_recv.at[d - 1, c],
                at(y_peer(d), z, core, v),
            )
            for d in range(1, ny)
        ])

    for copy in mom_copies:
        copy.wait_recv()
    total = mom_core[...]
    for d in range(1, ny):
        total = total + mom_y[d - 1]
    mom_y_sum[...] = total
    mom_copies = [
        send(mom_y_sum, mom_z.at[d - 1], mom_send.at[ny - 1 + d], mom_recv.at[ny - 1 + d], at(y, z_peer(d), core, v))
        for d in range(1, nz)
    ]

    z_copies = []
    for c in range(CHUNKS):
        cols = pl.ds(c * width, width)
        for copy in y_copies[c]:
            copy.wait_recv()
        total = chip_sum[pl.ds(pl.multiple_of(y * nz, 8), nz), cols]
        for d in range(1, ny):
            total = total + from_y[d - 1, :, cols]
        part_lanes = width // 128
        for j in range(part_lanes):
            for k in range(nz):
                y_sum[k, pl.ds(c * part_lanes + j, 1), :] = total[k : k + 1, j * 128 : (j + 1) * 128]
        lines = pl.ds(c * part_lanes, part_lanes)
        z_copies += [
            send(
                y_sum.at[z_peer(d), lines, :],
                from_z.at[d - 1, lines, :],
                z_send.at[d - 1, c],
                z_recv.at[d - 1, c],
                at(y, z_peer(d), core, v),
            )
            for d in range(1, nz)
        ]

    for copy in mom_copies:
        copy.wait_recv()
    moments = mom_y_sum[...]
    for d in range(1, nz):
        moments = moments + mom_z[d - 1]
    spread = moments[1] - moments[0] * moments[0] / samples + 1.0
    scale = jnp.sqrt(sigma2 * spread)
    for copy in z_copies:
        copy.wait_recv()
    total = y_sum[z]
    for d in range(1, nz):
        total = total + from_z[d - 1]
    statistic = total / scale
    stat_out[...] = statistic
    top[...] = jnp.broadcast_to(jnp.max(jnp.abs(statistic), keepdims=True), top.shape)
    x_copies = [
        send(top, from_x.at[d - 1], x_send.at[d - 1], x_recv.at[d - 1], at(y, z, core, x_peer(d)))
        for d in range(1, nx)
    ]
    for copy in x_copies:
        copy.wait_recv()
    largest = top[...]
    for d in range(1, nx):
        largest = jnp.maximum(largest, from_x[d - 1])
    max_out[...] = largest
    for copy in sent:
        copy.wait_send()


def solution(mesh):
    nx = mesh.shape["var"]
    ny, nz = 4, mesh.shape["samp"] // 8
    dims = (ny, nz, nx)

    def on_device(phenotype, perm_index, genotypes):
        perms, local = perm_index.shape
        columns = genotypes.shape[1]
        lanes = columns // 128
        samples = phenotype.shape[0]
        own = perms // nx
        anywhere = pl.BlockSpec(memory_space=pl.ANY)
        vmem = pl.BlockSpec(memory_space=pltpu.VMEM)
        dma = pltpu.SemaphoreType.DMA
        statistics, largest = pl.pallas_call(
            functools.partial(kernel, dims),
            out_shape=(
                jax.ShapeDtypeStruct((lanes, 128), F32),
                jax.ShapeDtypeStruct((1, 128), F32),
            ),
            in_specs=[anywhere] * 3,
            out_specs=(vmem, vmem),
            scratch_shapes=[
                pltpu.VMEM((samples // 128, 128), F32),
                pltpu.VMEM((256, 256), BF16),
                pltpu.VMEM((2 * own, local), jnp.int32),
                pltpu.VMEM((local, columns), BF16),
                pltpu.VMEM((perms, local), F32),
                pltpu.VMEM((perms, local), BF16),
                pltpu.VMEM((perms, columns), F32),
                pltpu.VMEM((perms // 2, columns), F32),
                pltpu.VMEM((perms // 2, columns), F32),
                pltpu.VMEM((ny - 1, nz, columns), F32),
                pltpu.VMEM((nz, lanes, 128), F32),
                pltpu.VMEM((nz - 1, lanes, 128), F32),
                pltpu.VMEM((2, lanes, 128), F32),
                pltpu.VMEM((2, lanes, 128), F32),
                pltpu.VMEM((ny - 1, 2, lanes, 128), F32),
                pltpu.VMEM((2, lanes, 128), F32),
                pltpu.VMEM((nz - 1, 2, lanes, 128), F32),
                pltpu.VMEM((1, 128), F32),
                pltpu.VMEM((nx - 1, 1, 128), F32),
                dma((2 + G_COPIES,)),
                dma((nx - 1, own // 8)),
                dma((nx - 1, own // 8)),
                dma((ny + nz - 1,)),
                dma((ny + nz - 1,)),
                dma((CHUNKS,)),
                dma((CHUNKS,)),
                dma((ny - 1, CHUNKS)),
                dma((ny - 1, CHUNKS)),
                dma((nz - 1, CHUNKS)),
                dma((nz - 1, CHUNKS)),
                dma((nx - 1,)),
                dma((nx - 1,)),
            ],
            compiler_params=pltpu.CompilerParams(
                collective_id=0, has_side_effects=True, vmem_limit_bytes=40 * 1024 * 1024
            ),
        )(phenotype.reshape(samples // 128, 128), perm_index, genotypes)
        return statistics.reshape(1, columns), largest[0, :1]

    return jax.shard_map(
        on_device,
        mesh=mesh,
        in_specs=(P(), P(None, "samp"), P("samp", "var")),
        out_specs=(P("samp", "var"), P("samp")),
        check_vma=False,
    )
```

time: 139 us -> 39.3 us (0.28)
  matrix products: 43.8 us -> 0 us
  waiting for transfers between devices: 40.5 us -> 0 us
  Pallas kernels: 0 us -> 32.4 us
  starting transfers between devices: 19.4 us -> 0 us
  other arithmetic: 19.2 us -> 0 us
  blocking collectives: 7.95 us -> 0 us
    dot_general x10 -> x0, matrix products: 43.8 us -> none  [the longest x8 37.8 us: select_rows(): jnp.einsum('pnh,hc->pnc', upper_part, table, preferred_element_type=jnp.f...]
    all_to_all x2 -> x0, waiting for transfers between devices: 40.5 us -> none  [the longest x1 27.6 us: from_everyone(): lax.all_to_all(jnp.broadcast_to(shard[None], (length, *shard.shape)), axi...]
    pallas_call x0 -> x1, Pallas kernels: none -> 32.4 us  [on_device(): pl.pallas_call(functools.partial(kernel, dims), out_shape=(jax.ShapeDtype...]
    all_to_all x2 -> x0, starting transfers between devices: 19.4 us -> none  [the longest x1 13.1 us: sent_and_summed(): lax.all_to_all(pieces, axis, split_axis=0, concat_axis=0, tiled=True)]
    select_n x16 -> x0, other arithmetic: 12.5 us -> none  [the longest x8 6.3 us: select_rows(): index_rows // 128]
    all_to_all x1 -> x0, blocking collectives: 7.95 us -> none  [from_everyone(): lax.all_to_all(jnp.broadcast_to(shard[None], (length, *shard.shape)), axi...]
    unnamed x2 -> x7, local copies, waits for them, and re-layouts: 0.45 us -> 4.68 us
    reduce_sum x4 -> x0, other arithmetic: 3.92 us -> none  [the longest x1 1.62 us: on_device(): sigma2 = jnp.mean(centred * centred) + 1e-05]
  transfers between devices with their start and end apart: 2 -> 0, of which waited for: 2 -> 0; matrix products, arithmetic and copies ran while one was open for 3% -> 0% of each run, Pallas kernels for 0% -> 0%
where the time goes in v1:
time: 39.3 us; the launch traced here: 38.9 us
  Pallas kernels  32.4 us (82%)
  local copies, waits for them, and re-layouts  4.68 us (12%)
  between operations  1.81 us (5%)
    pallas_call x1, Pallas kernels, on_device(): pl.pallas_call(functools.partial(kernel, dims), out_shape=(jax.ShapeDtype...  32.4 us
    unnamed x7, local copies, waits for them, and re-layouts  4.68 us

profile of v1, /device:TPU:1, one launch (start us, length us, event | category | flops | bytes accessed | tf_op | source)
XLA Modules:
  0.0 38.9 jit_solution(10342415821256751238)
XLA Ops:
  0.6 0.0 copy-start
  0.6 2.2 %copy-done = bf16[1024,2048]{1,0:T(8,128)(2,1)S(1)} copy-done((bf16[1024,2048]{1,0:T(8,128)(2,1)S(1)}, bf16[1024,2048]{1,0:T(8,128)(2,1)}, u32[]{:S(2)}) %copy-start) | copy-done | bytes 4194328
  2.8 0.0 copy-start.1
  2.8 0.9 %copy-done.1 = f32[65536]{0:T(1024)S(1)} copy-done((f32[65536]{0:T(1024)S(1)}, f32[65536]{0:T(1024)}, u32[]{:S(2)}) %copy-start.1) | copy-done | bytes 262168
  3.8 0.0 copy-start.2
  3.8 0.9 %copy-done.2 = s32[64,1024]{1,0:T(8,128)S(1)} copy-done((s32[64,1024]{1,0:T(8,128)S(1)}, s32[64,1024]{1,0:T(8,128)}, u32[]{:S(2)}) %copy-start.2) | copy-done | bytes 262168
  4.7 32.4 %shard_map.50 = (f32[16,128]{1,0:T(8,128)S(1)}, f32[1,128]{1,0:T(1,128)S(1)}) custom-call(f32[512,128]{1,0:T(8,128)S(1)} %bitcast.4, s32[64,1024]{1,0:T(8,128)S(1)} %copy-done.2, bf16[1024,2048]{1,0:T(8,128)(2,1)S(1)} %copy-done), custom_call_target="tpu_custom_call" | custom-call | tf_op jit(solution)/shard_map/pallas_call | solution.py:256
  37.1 0.6 %copy.7 = f32[1,2048]{1,0:T(1,128)} copy(f32[1,2048]{1,0:T(1,128)S(1)} %bitcast.5) | data formatting | bytes 16384
Async XLA Ops:
  0.6 2.2 %copy-start = (bf16[1024,2048]{1,0:T(8,128)(2,1)S(1)}, bf16[1024,2048]{1,0:T(8,128)(2,1)}, u32[]{:S(2)}) copy-start(bf16[1024,2048]{1,0:T(8,128)(2,1)} %g_hbm.1) | copy-start | bytes 12582916
  2.8 0.9 %copy-start.1 = (f32[65536]{0:T(1024)S(1)}, f32[65536]{0:T(1024)}, u32[]{:S(2)}) copy-start(f32[65536]{0:T(1024)} %param.3) | copy-start | bytes 786436
  3.8 0.9 %copy-start.2 = (s32[64,1024]{1,0:T(8,128)S(1)}, s32[64,1024]{1,0:T(8,128)}, u32[]{:S(2)}) copy-start(s32[64,1024]{1,0:T(8,128)} %idx_hbm.1) | copy-start | bytes 786436
